TPU v7x, 32 devices: a whole 2x2x4 slice. The times are simulated.
32 devices in a mesh: dp: 16 (over z, y, core), local: 2 (over x).
Axes of the slice: x: 2, y: 2, z: 4, core: 2. Of those that a mesh axis runs over, the one named last changes fastest.
Arguments:
- pre_glu: bfloat16 [32, 256, 3072], P(('dp', 'local')), may hold values from -80 to 80
- lengths: int32 [32], P(('dp', 'local')), may hold values from 1 to 256, as said below
- kernel: float32 [5, 1536], replicated, may hold values from -2.5 to 2.5
- bn_gain: float32 [1536], replicated, may hold values from 0.5 to 2
- bn_shift: float32 [1536], replicated, may hold values from -1 to 1
- w_out: bfloat16 [1536, 1536], replicated, may hold values from -0.15625 to 0.15625
- cotangent: bfloat16 [32, 256, 1536], P(('dp', 'local')), may hold values from -6 to 6
Outputs:
- grad_pre_glu: bfloat16 [32, 256, 3072], P(('dp', 'local'))
- grad_w_out: float32 [1536, 1536], P('dp', 'local')
- grad_kernel: float32 [5, 1536], replicated
- grad_gain: float32 [1536], replicated
- grad_shift: float32 [1536], replicated
Inputs may be any that keep to these rules, and one draw needn't show every extreme that they name: `lengths`: each utterance's valid frames are its first ones; some utterance has all 256 frames valid.
All inputs are finite; a program needn't handle non-finite values.
Results may differ from a plain program's by a relative error of at most 0.0029.
Values sent between devices are 32-bit elements; how exact they have to be, the bound alone decides.
A program may use at most 64 MiB of HBM per device.

v0:
```python
import jax
import jax.numpy as jnp
from jax import lax
from jax.sharding import PartitionSpec as P

epsilon = 1e-05


def on_device(pre_glu, lengths, kernel, bn_gain, bn_shift, w_out, cotangent):
    frames = pre_glu.shape[1]
    model_width = kernel.shape[1]
    kernel_taps = kernel.shape[0]
    half_width = (kernel_taps - 1) // 2
    replicas = lax.axis_size("dp") * lax.axis_size("local")
    valid_mask = (jnp.arange(frames, dtype=jnp.int32)[:, None] < lengths[0]).astype(jnp.float32)
    first_half = pre_glu[0, :, :model_width].astype(jnp.float32)
    gate_value = jax.nn.sigmoid(pre_glu[0, :, model_width:].astype(jnp.float32))
    glu_out = first_half * gate_value * valid_mask
    padded = jnp.pad(glu_out, ((half_width, half_width), (0, 0)))
    conv_out = kernel[0] * padded[0:frames]
    for j in range(1, kernel_taps):
        conv_out = conv_out + kernel[j] * padded[j : j + frames]
    own_count = lengths[0].astype(jnp.float32)
    sum_first, sum_square, frame_total = lax.psum(
        (
            jnp.sum(conv_out * valid_mask, 0),
            jnp.sum(conv_out * conv_out * valid_mask, 0),
            own_count,
        ),
        ("dp", "local"),
    )
    mean_value = sum_first / frame_total
    variance = sum_square / frame_total - mean_value * mean_value
    invstd = lax.rsqrt(variance + epsilon)
    normed = (conv_out - mean_value) * invstd
    act_in = bn_gain * normed + bn_shift
    sig_act = jax.nn.sigmoid(act_in)
    swished = (act_in * sig_act).astype(jnp.bfloat16)
    masked_cot = cotangent[0] * valid_mask.astype(jnp.bfloat16)
    contract = (((0,), (0,)), ((), ()))
    wgrad_term = lax.dot_general(swished, masked_cot, contract, preferred_element_type=jnp.float32)
    partial_value = lax.psum_scatter(wgrad_term, "dp", scatter_dimension=0, tiled=True)
    weight_shard = lax.psum_scatter(partial_value, "local", scatter_dimension=1, tiled=True)
    grad_swish = lax.dot_general(
        masked_cot, w_out, (((1,), (1,)), ((), ())), preferred_element_type=jnp.float32
    )
    grad_act = grad_swish * sig_act * (1.0 + act_in * (1.0 - sig_act))
    channel_scale = bn_gain * invstd
    sum_shift, sum_gain = lax.psum(
        (jnp.sum(grad_act, 0), jnp.sum(grad_act * normed, 0)), ("dp", "local")
    )
    grad_conv = (
        valid_mask * channel_scale * (grad_act - (sum_shift + normed * sum_gain) / frame_total)
    )
    kernel_part = jnp.stack(
        [jnp.sum(grad_conv * padded[j : j + frames], 0) for j in range(kernel_taps)], 0
    )
    kernel_sum = lax.psum(kernel_part, ("dp", "local"))
    grad_padded = jnp.pad(grad_conv, ((half_width, half_width), (0, 0)))
    grad_glu = kernel[0] * grad_padded[kernel_taps - 1 : kernel_taps - 1 + frames]
    for j in range(1, kernel_taps):
        grad_glu = (
            grad_glu + kernel[j] * grad_padded[kernel_taps - 1 - j : kernel_taps - 1 - j + frames]
        )
    grad_glu = grad_glu * valid_mask
    grad_first = grad_glu * gate_value
    grad_second = grad_glu * first_half * gate_value * (1.0 - gate_value)
    grad_pre = jnp.concatenate([grad_first, grad_second], 1).astype(jnp.bfloat16)[None]
    return (
        grad_pre,
        weight_shard / replicas,
        kernel_sum / replicas,
        sum_gain / replicas,
        sum_shift / replicas,
    )


def solution(mesh):
    return jax.shard_map(
        on_device,
        mesh=mesh,
        in_specs=(
            P(("dp", "local"), None, None),
            P(("dp", "local")),
            P(),
            P(),
            P(),
            P(),
            P(("dp", "local"), None, None),
        ),
        out_specs=(P(("dp", "local"), None, None), P("dp", "local"), P(), P(), P()),
        check_vma=False,
    )
```

profile of v0, /device:TPU:0, one launch (start us, length us, event | category | flops | bytes accessed | tf_op | source)
XLA Modules:
  0.0 228.4 jit_solution(6184416316779539486)
XLA Ops:
  7.2 0.0 reduce-scatter.3.cloned.1.call-start
  7.9 1.1 slice_reduce_fusion.4
  9.0 1.8 fusion.1
  10.8 0.0 copy-start.2
  10.8 0.0 copy-start.3
  10.8 1.1 multiply_reduce_fusion.7
  11.9 42.4 %all-reduce.3 = (f32[1536]{0:T(1024)S(1)}, f32[]{:T(128)}, f32[1536]{0:T(1024)S(1)}) all-reduce(f32[1536]{0:T(1024)S(1)} %get-tuple-element.11, f32[]{:T(128)S(6)} %convert_element_type.50, f32[1536]{0:T(1024)S(1)} %get-tuple-element.10), channel_id=1, replica_groups=mesh['dp'=16,'local'=2] {'dp','local'}, use_global_device_ids=true, to_apply=%region_4.5 | all-reduce | flops 3073 | bytes 24584 | tf_op jit(solution)/shard_map/psum | solution.py:24
  54.4 0.0 copy-done.2
  54.4 0.7 fusion.17
  55.0 0.7 add_rsqrt_fusion
  55.7 0.0 copy-done.3
  55.7 6.4 %fusion.7 = f32[1536,1536]{1,0:T(8,128)} fusion(f32[256,1536]{1,0:T(8,128)S(1)} %get-tuple-element.29, f32[1536]{0:T(1024)S(1)} %copy-done.3, f32[1536]{0:T(1024)S(1)} %add_rsqrt_fusion, f32[1536]{0:T(1024)S(1)} %get-tuple-element.28, f32[1536]{0:T(1024)S(1)} %copy-done.2, bf16[1,256,1536]{2,1,0:T(8,128)(2,1)} %param.13, bf16[256]{0:T(256)(128)(2,1)S(1)} %fusion.18), kind=kOutput, calls=%fused_computation.33 | convolution fusion | flops 1211891712 | bytes 11821568 | tf_op jit(solution)/shard_map/dot_general | solution.py:41
  62.1 0.0 reduce-scatter.3.cloned.1.call-update
  62.2 0.0 reduce-scatter.5.cloned.1.call-start
  62.2 5.6 %fusion.20 = (f32[1536]{0:T(1024)S(1)}, f32[1536]{0:T(1024)S(1)}, f32[256,1536]{1,0:T(8,128)}) fusion(f32[1536]{0:T(1024)S(1)} %add_rsqrt_fusion, f32[256,1536]{1,0:T(8,128)S(1)} %get-tuple-element.29, f32[1536]{0:T(1024)S(1)} %get-tuple-element.28, f32[1536]{0:T(1024)S(1)} %copy-done.3, f32[1536]{0:T(1024)S(1)} %copy-done.2, ...), kind=kOutput, calls=%fused_computation.60 | convolution fusion | flops 1214247936 | bytes 8688128 | tf_op jit(solution)/shard_map/dot_general | solution.py:44
  67.8 41.1 %all-reduce.2 = (f32[1536]{0:T(1024)S(1)}, f32[1536]{0:T(1024)S(1)}) all-reduce(f32[1536]{0:T(1024)S(1)} %get-tuple-element.13, f32[1536]{0:T(1024)S(1)} %get-tuple-element.12), channel_id=1, replica_groups=mesh['dp'=16,'local'=2] {'dp','local'}, use_global_device_ids=true, to_apply=%region_8.9 | all-reduce | flops 3072 | bytes 24576 | tf_op jit(solution)/shard_map/psum | solution.py:49
  108.9 0.0 copy-start
  108.9 3.5 %multiply_reduce_fusion = (f32[1536]{0:T(1024)S(1)}, f32[1536]{0:T(1024)S(1)}, f32[1536]{0:T(1024)S(1)}, f32[1536]{0:T(1024)S(1)}, f32[1536]{0:T(1024)S(1)}, /*index=5*/f32[256,1536]{1,0:T(8,128)S(1)}) fusion(f32[256,1536]{1,0:T(8,128)S(1)} %fusion.1, f32[256,1536]{1,0:T(8,128)} %get-tuple-element.30, f32[]{:T(128)} %get-tuple-element.22, ...), kind=kLoop, calls=%fused_computation.12 | loop fusion | flops 7070208 | bytes 6353924 | tf_op jit(solution)/shard_map/reduce_sum | solution.py:56
  112.4 0.0 copy-done
  112.4 0.0 copy-start.1
  112.4 2.2 fusion.8
  114.6 59.1 %reduce-scatter.3.cloned.1.call-done = f32[96,1536]{1,0:T(8,128)} async-done(((f32[1536,1536]{1,0:T(8,128)}), f32[96,1536]{1,0:T(8,128)}) %reduce-scatter.3.cloned.1.call-update) | async-done | bytes 589840 | tf_op jit(solution)/shard_map/reduce_scatter | solution.py:42
  173.7 0.0 reduce-scatter.5.cloned.1.call-update
  173.7 0.0 copy-done.1
  173.7 1.4 fusion.9
  175.2 0.1 stack.23
  175.2 40.7 %psum.47 = f32[5,1536]{1,0:T(8,128)S(1)} all-reduce(f32[5,1536]{1,0:T(8,128)S(1)} %stack.23), channel_id=1, replica_groups=mesh['dp'=16,'local'=2] {'dp','local'}, use_global_device_ids=true, to_apply=%region_16.17 | all-reduce | flops 7680 | bytes 61440 | tf_op jit(solution)/shard_map/psum | solution.py:58
  216.0 0.6 broadcast_multiply_fusion.2
  216.6 2.7 %pad_maximum_fusion = bf16[1,256,3072]{2,1,0:T(8,128)(2,1)} fusion(bf16[1,256,1536]{2,1,0:T(8,128)(2,1)} %fusion.9, bf16[1,256,1536]{2,1,0:T(8,128)(2,1)} %get-tuple-element.25), kind=kLoop, calls=%fused_computation.8 | loop fusion | flops 3145728 | bytes 3145728 | tf_op jit(solution)/shard_map/concatenate | solution.py:68
  219.2 0.6 broadcast_multiply_fusion.1
  219.9 0.0 reduce-scatter.5.cloned.1.call-done
  219.9 1.7 broadcast_multiply_fusion
  (7 shorter events, 0.0 us)
Async XLA Ops:
  7.2 166.5 %reduce-scatter.3.cloned.1.call-start = ((), (), s32[]{:S(2)}) async-start(), calls=%async_computation.2 | async-start | bytes 10027008 | tf_op jit(solution)/shard_map/reduce_scatter | solution.py:42
  10.8 43.6 %copy-start.2 = (f32[1536]{0:T(1024)S(1)}, f32[1536]{0:T(1024)}, u32[]{:S(2)}) copy-start(f32[1536]{0:T(1024)} %param.10) | copy-start | bytes 18436
  10.8 44.9 %copy-start.3 = (f32[1536]{0:T(1024)S(1)}, f32[1536]{0:T(1024)}, u32[]{:S(2)}) copy-start(f32[1536]{0:T(1024)} %param.11) | copy-start | bytes 18436
  62.2 157.7 %reduce-scatter.5.cloned.1.call-start = ((), (), s32[]{:S(2)}) async-start(), calls=%async_computation.3 | async-start | bytes 884736 | tf_op jit(solution)/shard_map/reduce_scatter | solution.py:43
  108.9 3.5 %copy-start = (bf16[1,256,3072]{2,1,0:T(8,128)(2,1)S(1)}, bf16[1,256,3072]{2,1,0:T(8,128)(2,1)}, u32[]{:S(2)}) copy-start(bf16[1,256,3072]{2,1,0:T(8,128)(2,1)} %param.7) | copy-start | bytes 4718596
  112.4 61.3 %copy-start.1 = (bf16[1,256,3072]{2,1,0:T(8,128)(2,1)S(1)}, bf16[1,256,3072]{2,1,0:T(8,128)(2,1)}, u32[]{:S(2)}) copy-start(bf16[1,256,3072]{2,1,0:T(8,128)(2,1)} %param.7) | copy-start | bytes 4718596
Sparse Core Ops, SparseCore 0:
  62.3 111.3 reduce-scatter.2
  175.9 15.2 reduce-scatter.4
where the time goes:
time: 229 us; the launch traced here: 228 us
  blocking collectives  124 us (54%)
  waiting for transfers between devices  59.1 us (26%)
  other arithmetic  16.9 us (7%)
  between operations  14.8 us (6%)
  matrix products  12 us (5%)
    reduce_scatter x1, waiting for transfers between devices, on_device(): lax.psum_scatter(wgrad_term, 'dp', scatter_dimension=0, tiled=True)  59.1 us
    psum x1, blocking collectives, on_device(): lax.psum((jnp.sum(conv_out * valid_mask, 0), jnp.sum(conv_out * conv_out...  42.4 us
    psum x1, blocking collectives, on_device(): lax.psum((jnp.sum(grad_act, 0), jnp.sum(grad_act * normed, 0)), ('dp', 'l...  41.1 us
    psum x1, blocking collectives, on_device(): kernel_sum = lax.psum(kernel_part, ('dp', 'local'))  40.7 us
    dot_general x1, matrix products, on_device(): lax.dot_general(swished, masked_cot, contract, preferred_element_type=jnp...  6.43 us
    concatenate x3, other arithmetic, on_device(): jnp.concatenate([grad_first, grad_second], 1).astype(jnp.bfloat16)[None]  6.24 us
    dot_general x1, matrix products, on_device(): lax.dot_general(masked_cot, w_out, (((1,), (1,)), ((), ())), preferred_el...  5.56 us
  transfers between devices with their start and end apart: 2, of which 1 were waited for; matrix products, arithmetic and copies ran while one was open for 7% of the time, Pallas kernels for 0%

commit v1 on v0

v1 whole, which is shorter than its diff:
```python
import functools

import jax
import jax.numpy as jnp
from jax import lax
from jax.experimental import pallas as pl
from jax.experimental.pallas import tpu as pltpu
from jax.sharding import PartitionSpec as P

epsilon = 1e-05
LANES = 128
EDGE = 8
MESH = pl.DeviceIdType.MESH
f32 = jnp.float32
bf16 = jnp.bfloat16


def split(count):
    factors = []
    while count > 1:
        wanted = (2,) if len(factors) < 2 else (4, 3, 2)
        wanted += tuple(range(2, count + 1))
        factor = next(f for f in wanted if count % f == 0)
        factors.append(factor)
        count //= factor
    return factors


class Plan:
    def __init__(self, dp, local, width, frames, taps):
        self.dp, self.local, self.width, self.frames, self.taps = dp, local, width, frames, taps
        digits, stride = [], 1
        for factor in split(dp):
            digits.append(("dp", stride, factor))
            stride *= factor
        across = ("local", 1, local)
        first, second, rest = digits[:1], digits[1:2], digits[2:]
        middle = second + ([across] if local > 1 else [])
        self.sum_groups = [g for g in [first, middle] + [[d] for d in rest] if g]
        self.rows, self.cols = width // dp, width // local
        self.chunks = self.cols // LANES
        orders = (first + middle[::-1] + rest, first + middle + rest)
        self.orders = [orders[k % 2] for k in range(self.chunks)]
        self.tiles = width // LANES
        self.up = lambda n: -(-n // 8) * 8
        self.sum_rows = [self.up(2 * self.tiles + 1), self.up(2 * self.tiles), self.up(taps * self.tiles)]

    def size(self, group):
        total = 1
        for _, _, count in group:
            total *= count
        return total

    def scratch(self):
        shapes, sems = [], 0
        for rows in self.sum_rows:
            shapes.append(pltpu.VMEM((rows, LANES), f32))
            for group in self.sum_groups:
                shapes.append(pltpu.VMEM((self.size(group), rows, LANES), f32))
                sems += self.size(group) - 1
        for order in self.orders:
            blocks = self.dp * self.local
            shapes.append(pltpu.VMEM((blocks, self.rows, LANES), f32))
            for digit in order:
                blocks //= digit[2]
                shapes.append(pltpu.VMEM((digit[2] - 1, blocks, self.rows, LANES), f32))
                sems += digit[2] - 1
        return shapes, sems


class Here:
    def __init__(self):
        self.at = {"dp": lax.axis_index("dp"), "local": lax.axis_index("local")}

    def digit(self, part):
        axis, stride, size = part
        return lax.rem(lax.div(self.at[axis], jnp.int32(stride)), jnp.int32(size))

    def index(self, group):
        total = jnp.int32(0)
        for part in group:
            total = total * part[2] + self.digit(part)
        return total

    def device(self, group, member):
        place = dict(self.at)
        for part in reversed(group):
            axis, stride, size = part
            wanted = lax.rem(member, jnp.int32(size))
            member = lax.div(member, jnp.int32(size))
            place[axis] = place[axis] + (wanted - self.digit(part)) * stride
        return (place["dp"], place["local"])


class Wire:
    def __init__(self, send, recv):
        self.send, self.recv, self.next, self.all = send, recv, 0, []

    def start(self, src, dst, device):
        copy = pltpu.make_async_remote_copy(
            src_ref=src,
            dst_ref=dst,
            send_sem=self.send.at[self.next],
            recv_sem=self.recv.at[self.next],
            device_id=device,
            device_id_type=MESH,
        )
        self.next += 1
        copy.start()
        self.all.append(copy)
        return copy


class Total:
    def __init__(self, plan, here, wire, refs):
        self.groups, self.here, self.wire = plan.sum_groups, here, wire
        self.total, self.slots = refs[0], refs[1:]
        self.copies = None
        self.size = plan.size

    def send(self, stage):
        group, slots = self.groups[stage], self.slots[stage]
        mine, count = self.here.index(group), self.size(group)
        slots[mine] = self.total[...]
        self.copies = [
            self.wire.start(
                slots.at[mine],
                slots.at[mine],
                self.here.device(group, lax.rem(mine + k, jnp.int32(count))),
            )
            for k in range(1, count)
        ]

    def take(self, stage):
        slots = self.slots[stage]
        for copy in self.copies:
            copy.wait_recv()
        value = slots[0]
        for k in range(1, self.size(self.groups[stage])):
            value = value + slots[k]
        self.total[...] = value


class Scatter:
    def __init__(self, order, here, wire, refs):
        self.order, self.here, self.wire = order, here, wire
        self.held, self.landing = [refs[0]], refs[1:]
        self.held += [slot.at[0] for slot in self.landing]
        self.copies = None

    def send(self, stage):
        digit, landing = self.order[stage], self.landing[stage]
        mine, count, blocks = self.here.digit(digit), digit[2], landing.shape[1]
        self.copies = []
        for k in range(1, count):
            member = lax.rem(mine + k, jnp.int32(count))
            self.copies.append(
                self.wire.start(
                    self.held[stage].at[pl.ds(member * blocks, blocks)],
                    landing.at[k - 1],
                    self.here.device([digit], member),
                )
            )

    def take(self, stage):
        digit, landing, held = self.order[stage], self.landing[stage], self.held[stage]
        mine, count, blocks = self.here.digit(digit), digit[2], landing.shape[1]
        for copy in self.copies:
            copy.wait_recv()

        def add(b, carry):
            value = held[mine * blocks + b]
            for k in range(count - 1):
                value = value + landing[k, b]
            landing[0, b] = value
            return carry

        lax.fori_loop(0, blocks, add, 0)


def module_kernel(plan, count_sems, *refs):
    (length_ref, pre_ref, taps_ref, gain_ref, shift_ref, w_hbm, cot_hbm) = refs[:7]
    (pre_out, weight_out, taps_out, gain_out, shift_out) = refs[7:12]
    (w_ref, cot_ref, glu, conv, swish_t, arriving, conv_grad, pre_grad, local_sems, send, recv) = refs[12:23]
    pool = list(refs[23:])
    frames, width, taps, tiles = plan.frames, plan.width, plan.taps, plan.tiles
    half = (taps - 1) // 2
    here, wire = Here(), Wire(send, recv)

    w_copy = pltpu.make_async_copy(w_hbm, w_ref, local_sems.at[0])
    cot_copy = pltpu.make_async_copy(cot_hbm.at[0], cot_ref, local_sems.at[1])
    cot_copy.start()
    w_copy.start()

    barrier = pltpu.get_barrier_semaphore()
    peers = 0
    for group in plan.sum_groups:
        for k in range(1, plan.size(group)):
            member = lax.rem(here.index(group) + k, jnp.int32(plan.size(group)))
            pl.semaphore_signal(barrier, inc=1, device_id=here.device(group, member), device_id_type=MESH)
            peers += 1

    totals = []
    for _ in plan.sum_rows:
        take = 1 + len(plan.sum_groups)
        totals.append(Total(plan, here, wire, pool[:take]))
        pool = pool[take:]
    scatters = []
    for order in plan.orders:
        take = 1 + len(order)
        scatters.append(Scatter(order, here, wire, pool[:take]))
        pool = pool[take:]

    length = length_ref[0]
    rows_at = lax.broadcasted_iota(jnp.int32, (frames, LANES), 0)

    def valid():
        return jnp.where(rows_at < length, jnp.float32(1), jnp.float32(0))

    def at(tile, base=0):
        return pl.ds(pl.multiple_of(base + tile * LANES, LANES), LANES)

    def row(ref, r):
        return ref[pl.ds(r, 1), :]

    def column_sum(value):
        return jnp.sum(value, 0, keepdims=True)

    for ref in (glu, conv_grad):
        ref[0:EDGE, :] = jnp.zeros((EDGE, width), f32)
        ref[EDGE + frames :, :] = jnp.zeros((EDGE, width), f32)
    for total in totals:
        total.total[...] = jnp.zeros(total.total.shape, f32)

    stats = totals[0].total

    def front(tile, carry):
        cols = at(tile)
        mask = valid()
        first = pre_ref[0, :, cols].astype(f32)
        gate = jax.nn.sigmoid(pre_ref[0, :, at(tile, width)].astype(f32))
        glu[EDGE : EDGE + frames, cols] = first * gate * mask
        out = taps_ref[0:1, cols] * glu[EDGE - half : EDGE - half + frames, cols]
        for j in range(1, taps):
            start = EDGE + j - half
            out = out + taps_ref[j : j + 1, cols] * glu[start : start + frames, cols]
        conv[:, cols] = out
        kept = out * mask
        stats[pl.ds(tile, 1), :] = column_sum(kept)
        stats[pl.ds(tiles + tile, 1), :] = column_sum(out * kept)
        return carry

    lax.fori_loop(0, tiles, front, 0)
    stats[2 * tiles : 2 * tiles + 1, :] = jnp.full((1, LANES), length, jnp.int32).astype(f32)

    pl.semaphore_wait(barrier, peers)
    stages = len(plan.sum_groups)
    totals[0].send(0)
    cot_copy.wait()

    def mask_cot(tile, carry):
        cols = at(tile)
        cot_ref[:, cols] = (cot_ref[:, cols].astype(f32) * valid()).astype(bf16)
        return carry

    lax.fori_loop(0, tiles, mask_cot, 0)
    totals[0].take(0)
    totals[0].send(1)
    w_copy.wait()

    wide = 2 * LANES if tiles % 2 == 0 else LANES

    def back_matmul(tile, carry):
        cols = pl.ds(pl.multiple_of(tile * wide, wide), wide)
        arriving[:, cols] = lax.dot_general(
            cot_ref[...], w_ref[cols, :], (((1,), (1,)), ((), ())), preferred_element_type=f32
        )
        return carry

    lax.fori_loop(0, width // wide, back_matmul, 0)
    totals[0].take(1)
    for stage in range(2, stages):
        totals[0].send(stage)
        totals[0].take(stage)

    def moments(tile):
        count = row(stats, 2 * tiles)
        mean = row(stats, tile) / count
        variance = row(stats, tiles + tile) / count - mean * mean
        return count, mean, lax.rsqrt(variance + epsilon)

    sums = totals[1].total

    def activate(tile, carry):
        cols = at(tile)
        _, mean, invstd = moments(tile)
        normed = (conv[:, cols] - mean) * invstd
        act = gain_ref[0:1, cols] * normed + shift_ref[0:1, cols]
        sig = jax.nn.sigmoid(act)
        swish_t[cols, :] = (act * sig).T.astype(bf16)
        grad = arriving[:, cols] * sig * (1.0 + act * (1.0 - sig))
        arriving[:, cols] = grad
        sums[pl.ds(tile, 1), :] = column_sum(grad)
        sums[pl.ds(tiles + tile, 1), :] = column_sum(grad * normed)
        return carry

    lax.fori_loop(0, tiles, activate, 0)
    totals[1].send(0)

    def weight_chunk(k):
        scatter = scatters[k]
        parts = [
            cot_ref[:, c * plan.cols + k * LANES : c * plan.cols + (k + 1) * LANES]
            for c in range(plan.local)
        ]
        product = jnp.dot(swish_t[...], jnp.concatenate(parts, 1), preferred_element_type=f32)
        for d in range(plan.dp):
            for c in range(plan.local):
                block = 0
                for axis, stride, size in scatter.order:
                    block = block * size + ((d if axis == "dp" else c) // stride) % size
                scatter.held[0][block] = product[
                    d * plan.rows : (d + 1) * plan.rows, c * LANES : (c + 1) * LANES
                ]
        scatter.send(0)

    chunks = plan.chunks
    steps = len(plan.orders[0])
    for k in range(min(2, chunks)):
        weight_chunk(k)
    totals[1].take(0)
    totals[1].send(1)
    for k in range(min(2, chunks)):
        scatters[k].take(0)
        scatters[k].send(1)
    for k in range(2, chunks):
        weight_chunk(k)
    totals[1].take(1)
    for stage in range(2, stages):
        totals[1].send(stage)
        if stage == 2:
            for k in range(2, chunks):
                scatters[k].take(0)
                scatters[k].send(1)
        totals[1].take(stage)

    kernel_sums = totals[2].total

    def finish(tile, carry):
        cols = at(tile)
        mask = valid()
        count, mean, invstd = moments(tile)
        normed = (conv[:, cols] - mean) * invstd
        grad = (
            mask
            * (gain_ref[0:1, cols] * invstd)
            * (arriving[:, cols] - (row(sums, tile) + normed * row(sums, tiles + tile)) / count)
        )
        conv_grad[EDGE : EDGE + frames, cols] = grad
        back = jnp.zeros((frames, LANES), f32)
        for j in range(taps):
            start = EDGE + j - half
            kernel_sums[pl.ds(j * tiles + tile, 1), :] = column_sum(
                grad * glu[start : start + frames, cols]
            )
            start = EDGE + half - j
            back = back + taps_ref[j : j + 1, cols] * conv_grad[start : start + frames, cols]
        first = pre_ref[0, :, cols].astype(f32)
        gate = jax.nn.sigmoid(pre_ref[0, :, at(tile, width)].astype(f32))
        back = back * mask * gate
        pre_grad[:, cols] = back.astype(bf16)
        pre_grad[:, at(tile, width)] = (back * first * (1.0 - gate)).astype(bf16)
        return carry

    lax.fori_loop(0, tiles, finish, 0)
    out_copy = pltpu.make_async_copy(pre_grad, pre_out.at[0], local_sems.at[2])
    out_copy.start()
    replicas = plan.dp * plan.local
    totals[2].send(0)
    for t in range(tiles):
        cols = slice(t * LANES, (t + 1) * LANES)
        shift_out[0:1, cols] = sums[t : t + 1, :] / replicas
        gain_out[0:1, cols] = sums[tiles + t : tiles + t + 1, :] / replicas
    totals[2].take(0)
    totals[2].send(1)
    for k in range(chunks):
        scatters[k].take(1)
        scatters[k].send(2)
    totals[2].take(1)
    for stage in range(2, stages):
        totals[2].send(stage)
        for k in range(chunks):
            if stage + 1 < steps:
                scatters[k].take(stage)
                scatters[k].send(stage + 1)
        totals[2].take(stage)
    for t in range(tiles):
        cols = slice(t * LANES, (t + 1) * LANES)
        for j in range(taps):
            at_row = j * tiles + t
            taps_out[j : j + 1, cols] = kernel_sums[at_row : at_row + 1, :] / replicas
    for k in range(chunks):
        scatters[k].take(steps - 1)
        weight_out[:, k * LANES : (k + 1) * LANES] = scatters[k].landing[steps - 1][0, 0] / replicas
    for copy in wire.all:
        copy.wait_send()
    out_copy.wait()


def on_device(pre_glu, lengths, kernel, bn_gain, bn_shift, w_out, cotangent):
    frames, taps, width = pre_glu.shape[1], kernel.shape[0], kernel.shape[1]
    plan = Plan(lax.axis_size("dp"), lax.axis_size("local"), width, frames, taps)
    pool, sems = plan.scratch()
    vmem, anywhere = pl.BlockSpec(memory_space=pltpu.VMEM), pl.BlockSpec(memory_space=pl.ANY)
    smem = pl.BlockSpec(memory_space=pltpu.SMEM)
    grad_pre, weight, kernel_grad, gain_grad, shift_grad = pl.pallas_call(
        functools.partial(module_kernel, plan, sems),
        out_shape=(
            jax.ShapeDtypeStruct(pre_glu.shape, bf16),
            jax.ShapeDtypeStruct((plan.rows, plan.cols), f32),
            jax.ShapeDtypeStruct((taps, width), f32),
            jax.ShapeDtypeStruct((1, width), f32),
            jax.ShapeDtypeStruct((1, width), f32),
        ),
        in_specs=[smem, vmem, vmem, vmem, vmem, anywhere, anywhere],
        out_specs=(anywhere, vmem, vmem, vmem, vmem),
        scratch_shapes=[
            pltpu.VMEM((width, width), bf16),
            pltpu.VMEM((frames, width), bf16),
            pltpu.VMEM((frames + 2 * EDGE, width), f32),
            pltpu.VMEM((frames, width), f32),
            pltpu.VMEM((width, frames), bf16),
            pltpu.VMEM((frames, width), f32),
            pltpu.VMEM((frames + 2 * EDGE, width), f32),
            pltpu.VMEM((frames, 2 * width), bf16),
            pltpu.SemaphoreType.DMA((3,)),
            pltpu.SemaphoreType.DMA((sems,)),
            pltpu.SemaphoreType.DMA((sems,)),
        ]
        + pool,
        compiler_params=pltpu.CompilerParams(
            collective_id=0, has_side_effects=True, vmem_limit_bytes=60 * 1024 * 1024
        ),
    )(lengths, pre_glu, kernel, bn_gain[None], bn_shift[None], w_out, cotangent)
    return grad_pre, weight, kernel_grad, gain_grad[0], shift_grad[0]


def solution(mesh):
    return jax.shard_map(
        on_device,
        mesh=mesh,
        in_specs=(
            P(("dp", "local"), None, None),
            P(("dp", "local")),
            P(),
            P(),
            P(),
            P(),
            P(("dp", "local"), None, None),
        ),
        out_specs=(P(("dp", "local"), None, None), P("dp", "local"), P(), P(), P()),
        check_vma=False,
    )
```

time: 229 us -> 92.7 us (0.40)
  blocking collectives: 124 us -> 0 us
  Pallas kernels: 0 us -> 81.8 us
  waiting for transfers between devices: 59.1 us -> 0 us
  other arithmetic: 16.9 us -> 2.62 us
  between operations: 14.8 us -> 1.29 us
  matrix products: 12 us -> 0 us
  local copies, waits for them, and re-layouts: 1.21 us -> 6.63 us
    psum x3 -> x0, blocking collectives: 124 us -> none  [the longest x1 42.4 us: on_device(): lax.psum((jnp.sum(conv_out * valid_mask, 0), jnp.sum(conv_out * conv_out...]
    pallas_call x0 -> x1, Pallas kernels: none -> 81.8 us  [on_device(): pl.pallas_call(functools.partial(module_kernel, plan, sems), out_shape=(j...]
    reduce_scatter x2 -> x0, waiting for transfers between devices: 59.1 us -> none  [the longest x1 59.1 us: on_device(): lax.psum_scatter(wgrad_term, 'dp', scatter_dimension=0, tiled=True)]
    dot_general x2 -> x0, matrix products: 12 us -> none  [the longest x1 6.43 us: on_device(): lax.dot_general(swished, masked_cot, contract, preferred_element_type=jnp...]
    concatenate x3 -> x0, other arithmetic: 6.24 us -> none  [on_device(): jnp.concatenate([grad_first, grad_second], 1).astype(jnp.bfloat16)[None]]
    reduce_sum x2 -> x0, other arithmetic: 4.66 us -> none  [the longest x1 3.51 us: on_device(): jnp.sum(grad_conv * padded[j:j + frames], 0)]
    unnamed x8 -> x7, local copies, waits for them, and re-layouts: 0.02 us -> 4.04 us
    div x3 -> x0, other arithmetic: 2.93 us -> none  [the longest x1 1.69 us: on_device(): weight_shard / replicas]
  transfers between devices with their start and end apart: 2 -> 0, of which waited for: 1 -> 0; matrix products, arithmetic and copies ran while one was open for 7% -> 0% of each run, Pallas kernels for 0% -> 0%
where the time goes in v1:
time: 92.7 us; the launch traced here: 92.3 us
  Pallas kernels  81.8 us (88%)
  local copies, waits for them, and re-layouts  6.63 us (7%)
  other arithmetic  2.62 us (3%)
  between operations  1.29 us (1%)
    pallas_call x1, Pallas kernels, on_device(): pl.pallas_call(functools.partial(module_kernel, plan, sems), out_shape=(j...  81.8 us
    unnamed x7, local copies, waits for them, and re-layouts  4.04 us
    pallas_call x2, other arithmetic, on_device(): pl.pallas_call(functools.partial(module_kernel, plan, sems), out_shape=(j...  2.62 us

profile of v1, /device:TPU:0, one launch (start us, length us, event | category | flops | bytes accessed | tf_op | source)
XLA Modules:
  0.0 92.3 jit_solution(13526327066600176653)
XLA Ops:
  1.3 1.3 %broadcast_in_dim.6.refs_3_ = f32[1,1536]{1,0:T(1,128)} reshape(f32[1536]{0:T(1024)} %param.10) | data formatting | bytes 12288 | tf_op jit(solution)/shard_map/broadcast_in_dim | solution.py:444
  2.6 1.3 %broadcast_in_dim.7.refs_4_ = f32[1,1536]{1,0:T(1,128)} reshape(f32[1536]{0:T(1024)} %param.11) | data formatting | bytes 12288 | tf_op jit(solution)/shard_map/broadcast_in_dim | solution.py:444
  3.9 81.8 %shard_map.110 = (bf16[1,256,3072]{2,1,0:T(8,128)(2,1)}, f32[96,768]{1,0:T(8,128)}, f32[5,1536]{1,0:T(8,128)}, f32[1,1536]{1,0:T(1,128)}, f32[1,1536]{1,0:T(1,128)}) custom-call(s32[1]{0:T(128)S(6)} %copy.15.refs_0_, bf16[1,256,3072]{2,1,0:T(8,128)(2,1)} %refs_1_.1, f32[5,1536]{1,0:T(8,128)} %refs_2_.1, f32[1,1536]{1,0:T(1,128)} %broadcast_in_dim.6.refs_3_, ...), custom_call_target="tpu_custom_call" | custom-call | tf_op jit(solution)/shard_map/pallas_call | solution.py:416
  85.7 1.3 %reduce = f32[1536]{0:T(1024)} reduce(f32[1,1536]{1,0:T(1,128)} %get-tuple-element.13, f32[]{:T(128)} %constant.3), dimensions={0}, to_apply=%get-tuple-element.13.reduce_sub_computation | reduce | bytes 12292 | tf_op jit(solution)/shard_map/pallas_call | solution.py:416
  87.0 1.3 %reduce.1 = f32[1536]{0:T(1024)} reduce(f32[1,1536]{1,0:T(1,128)} %get-tuple-element.14, f32[]{:T(128)} %constant.3), dimensions={0}, to_apply=%get-tuple-element.14.reduce_sub_computation | reduce | bytes 12292 | tf_op jit(solution)/shard_map/pallas_call | solution.py:416
  88.3 0.0 copy-start
  88.3 0.0 copy-start.1
  88.3 2.7 %copy.16 = bf16[1,256,3072]{2,1,0:T(8,128)(2,1)} copy(bf16[1,256,3072]{2,1,0:T(8,128)(2,1)} %get-tuple-element.20) | data formatting | bytes 3145728
  91.0 0.0 copy-done
  91.0 0.7 copy.17
  91.7 0.0 copy-done.1
  91.7 0.6 copy.18
Async XLA Ops:
  88.3 2.7 %copy-start = (f32[96,768]{1,0:T(8,128)S(1)}, f32[96,768]{1,0:T(8,128)}, u32[]{:S(2)}) copy-start(f32[96,768]{1,0:T(8,128)} %get-tuple-element.21) | copy-start | bytes 884740
  88.3 3.4 %copy-start.1 = (f32[5,1536]{1,0:T(8,128)S(1)}, f32[5,1536]{1,0:T(8,128)}, u32[]{:S(2)}) copy-start(f32[5,1536]{1,0:T(8,128)} %get-tuple-element.22) | copy-start | bytes 92164

commit v2 on v1

--- a/solution.py
+++ b/solution.py
@@ -39,8 +39,19 @@
         self.sum_groups = [g for g in [first, middle] + [[d] for d in rest] if g]
         self.rows, self.cols = width // dp, width // local
         self.chunks = self.cols // LANES
-        orders = (first + middle[::-1] + rest, first + middle + rest)
-        self.orders = [orders[k % 2] for k in range(self.chunks)]
+        early = (first + middle[1:] + rest + middle[:1], first + middle[:1] + rest + middle[1:])
+        late = (first + middle[::-1] + rest, first + middle + rest)
+        self.halves = 2 if self.rows % 16 == 0 else 1
+        self.part = self.rows // self.halves
+        self.pieces, self.orders, self.jobs = {}, [], []
+        for low in range(0, self.chunks, 2):
+            for part in range(self.halves):
+                job = []
+                for chunk in range(low, min(low + 2, self.chunks)):
+                    job.append(len(self.orders))
+                    self.pieces[chunk, part] = len(self.orders)
+                    self.orders.append((early if low == 0 else late)[chunk % 2])
+                self.jobs.append(job)
         self.tiles = width // LANES
         self.up = lambda n: -(-n // 8) * 8
         self.sum_rows = [self.up(2 * self.tiles + 1), self.up(2 * self.tiles), self.up(taps * self.tiles)]
@@ -60,10 +71,10 @@
                 sems += self.size(group) - 1
         for order in self.orders:
             blocks = self.dp * self.local
-            shapes.append(pltpu.VMEM((blocks, self.rows, LANES), f32))
+            shapes.append(pltpu.VMEM((blocks, self.part, LANES), f32))
             for digit in order:
                 blocks //= digit[2]
-                shapes.append(pltpu.VMEM((digit[2] - 1, blocks, self.rows, LANES), f32))
+                shapes.append(pltpu.VMEM((digit[2] - 1, blocks, self.part, LANES), f32))
                 sems += digit[2] - 1
         return shapes, sems
 
@@ -115,7 +126,7 @@
     def __init__(self, plan, here, wire, refs):
         self.groups, self.here, self.wire = plan.sum_groups, here, wire
         self.total, self.slots = refs[0], refs[1:]
-        self.copies = None
+        self.copies, self.stage = None, -1
         self.size = plan.size
 
     def send(self, stage):
@@ -140,13 +151,33 @@
             value = value + slots[k]
         self.total[...] = value
 
+    def advance(self):
+        if self.stage == len(self.groups):
+            return False
+        if self.stage >= 0:
+            self.take(self.stage)
+        self.stage += 1
+        if self.stage < len(self.groups):
+            self.send(self.stage)
+        return True
+
 
 class Scatter:
     def __init__(self, order, here, wire, refs):
         self.order, self.here, self.wire = order, here, wire
         self.held, self.landing = [refs[0]], refs[1:]
         self.held += [slot.at[0] for slot in self.landing]
-        self.copies = None
+        self.copies, self.stage = None, -1
+
+    def advance(self):
+        if self.stage == len(self.order):
+            return False
+        if self.stage >= 0:
+            self.take(self.stage)
+        self.stage += 1
+        if self.stage < len(self.order):
+            self.send(self.stage)
+        return True
 
     def send(self, stage):
         digit, landing = self.order[stage], self.landing[stage]
@@ -222,6 +253,9 @@
 
     def row(ref, r):
         return ref[pl.ds(r, 1), :]
+
+    def wide_row(ref, tile):
+        return ref[at(tile)].reshape(1, LANES)
 
     def column_sum(value):
         return jnp.sum(value, 0, keepdims=True)
@@ -254,8 +288,7 @@
     stats[2 * tiles : 2 * tiles + 1, :] = jnp.full((1, LANES), length, jnp.int32).astype(f32)
 
     pl.semaphore_wait(barrier, peers)
-    stages = len(plan.sum_groups)
-    totals[0].send(0)
+    totals[0].advance()
     cot_copy.wait()
 
     def mask_cot(tile, carry):
@@ -264,8 +297,7 @@
         return carry
 
     lax.fori_loop(0, tiles, mask_cot, 0)
-    totals[0].take(0)
-    totals[0].send(1)
+    totals[0].advance()
     w_copy.wait()
 
     wide = 2 * LANES if tiles % 2 == 0 else LANES
@@ -278,10 +310,8 @@
         return carry
 
     lax.fori_loop(0, width // wide, back_matmul, 0)
-    totals[0].take(1)
-    for stage in range(2, stages):
-        totals[0].send(stage)
-        totals[0].take(stage)
+    while totals[0].advance():
+        pass
 
     def moments(tile):
         count = row(stats, 2 * tiles)
@@ -291,58 +321,73 @@
 
     sums = totals[1].total
 
-    def activate(tile, carry):
+    def normed_act(tile):
         cols = at(tile)
         _, mean, invstd = moments(tile)
         normed = (conv[:, cols] - mean) * invstd
-        act = gain_ref[0:1, cols] * normed + shift_ref[0:1, cols]
-        sig = jax.nn.sigmoid(act)
-        swish_t[cols, :] = (act * sig).T.astype(bf16)
+        act = wide_row(gain_ref, tile) * normed + wide_row(shift_ref, tile)
+        return normed, act, jax.nn.sigmoid(act)
+
+    def activate(tile, carry):
+        _, act, sig = normed_act(tile)
+        swish_t[at(tile), :] = (act * sig).T.astype(bf16)
+        return carry
+
+    def act_grad(tile, carry):
+        cols = at(tile)
+        normed, act, sig = normed_act(tile)
         grad = arriving[:, cols] * sig * (1.0 + act * (1.0 - sig))
         arriving[:, cols] = grad
         sums[pl.ds(tile, 1), :] = column_sum(grad)
         sums[pl.ds(tiles + tile, 1), :] = column_sum(grad * normed)
         return carry
 
-    lax.fori_loop(0, tiles, activate, 0)
-    totals[1].send(0)
-
     def weight_chunk(k):
-        scatter = scatters[k]
+        if k >= plan.chunks:
+            return
         parts = [
             cot_ref[:, c * plan.cols + k * LANES : c * plan.cols + (k + 1) * LANES]
             for c in range(plan.local)
         ]
         product = jnp.dot(swish_t[...], jnp.concatenate(parts, 1), preferred_element_type=f32)
-        for d in range(plan.dp):
-            for c in range(plan.local):
-                block = 0
-                for axis, stride, size in scatter.order:
-                    block = block * size + ((d if axis == "dp" else c) // stride) % size
-                scatter.held[0][block] = product[
-                    d * plan.rows : (d + 1) * plan.rows, c * LANES : (c + 1) * LANES
-                ]
-        scatter.send(0)
-
-    chunks = plan.chunks
-    steps = len(plan.orders[0])
-    for k in range(min(2, chunks)):
+        for part in range(plan.halves):
+            scatter = scatters[plan.pieces[k, part]]
+            for d in range(plan.dp):
+                for c in range(plan.local):
+                    block = 0
+                    for axis, stride, size in scatter.order:
+                        block = block * size + ((d if axis == "dp" else c) // stride) % size
+                    low = d * plan.rows + part * plan.part
+                    scatter.held[0][block] = product[
+                        low : low + plan.part, c * LANES : (c + 1) * LANES
+                    ]
+            scatter.advance()
+
+    def go(*jobs):
+        for job in jobs:
+            if job < len(plan.jobs):
+                for piece in plan.jobs[job]:
+                    scatters[piece].advance()
+
+    lax.fori_loop(0, tiles, activate, 0)
+    weight_chunk(0)
+    weight_chunk(1)
+    lax.fori_loop(0, tiles, act_grad, 0)
+    totals[1].advance()
+    go(0)
+    totals[1].advance()
+    go(1)
+    weight_chunk(2)
+    weight_chunk(3)
+    totals[1].advance()
+    go(0)
+    weight_chunk(4)
+    weight_chunk(5)
+    for k in range(6, plan.chunks):
         weight_chunk(k)
-    totals[1].take(0)
-    totals[1].send(1)
-    for k in range(min(2, chunks)):
-        scatters[k].take(0)
-        scatters[k].send(1)
-    for k in range(2, chunks):
-        weight_chunk(k)
-    totals[1].take(1)
-    for stage in range(2, stages):
-        totals[1].send(stage)
-        if stage == 2:
-            for k in range(2, chunks):
-                scatters[k].take(0)
-                scatters[k].send(1)
-        totals[1].take(stage)
+    go(2, 3)
+    while totals[1].advance():
+        pass
 
     kernel_sums = totals[2].total
 
@@ -353,7 +398,7 @@
         normed = (conv[:, cols] - mean) * invstd
         grad = (
             mask
-            * (gain_ref[0:1, cols] * invstd)
+            * (wide_row(gain_ref, tile) * invstd)
             * (arriving[:, cols] - (row(sums, tile) + normed * row(sums, tiles + tile)) / count)
         )
         conv_grad[EDGE : EDGE + frames, cols] = grad
@@ -376,32 +421,29 @@
     out_copy = pltpu.make_async_copy(pre_grad, pre_out.at[0], local_sems.at[2])
     out_copy.start()
     replicas = plan.dp * plan.local
-    totals[2].send(0)
+    totals[2].advance()
+    go(1, 4)
+    totals[2].advance()
     for t in range(tiles):
         cols = slice(t * LANES, (t + 1) * LANES)
-        shift_out[0:1, cols] = sums[t : t + 1, :] / replicas
-        gain_out[0:1, cols] = sums[tiles + t : tiles + t + 1, :] / replicas
-    totals[2].take(0)
-    totals[2].send(1)
-    for k in range(chunks):
-        scatters[k].take(1)
-        scatters[k].send(2)
-    totals[2].take(1)
-    for stage in range(2, stages):
-        totals[2].send(stage)
-        for k in range(chunks):
-            if stage + 1 < steps:
-                scatters[k].take(stage)
-                scatters[k].send(stage + 1)
-        totals[2].take(stage)
+        shift_out[cols] = (sums[t : t + 1, :] / replicas).reshape(LANES)
+        gain_out[cols] = (sums[tiles + t : tiles + t + 1, :] / replicas).reshape(LANES)
+    go(2, 3, 5, 0, 2)
+    totals[2].advance()
+    go(1, 3, 4, 5, 4, 5)
+    while totals[2].advance():
+        pass
     for t in range(tiles):
         cols = slice(t * LANES, (t + 1) * LANES)
         for j in range(taps):
             at_row = j * tiles + t
             taps_out[j : j + 1, cols] = kernel_sums[at_row : at_row + 1, :] / replicas
-    for k in range(chunks):
-        scatters[k].take(steps - 1)
-        weight_out[:, k * LANES : (k + 1) * LANES] = scatters[k].landing[steps - 1][0, 0] / replicas
+    while any([scatter.advance() for scatter in scatters]):
+        pass
+    for (chunk, part), piece in plan.pieces.items():
+        weight_out[
+            part * plan.part : (part + 1) * plan.part, chunk * LANES : (chunk + 1) * LANES
+        ] = scatters[piece].landing[-1][0, 0] / replicas
     for copy in wire.all:
         copy.wait_send()
     out_copy.wait()
@@ -419,8 +461,8 @@
             jax.ShapeDtypeStruct(pre_glu.shape, bf16),
             jax.ShapeDtypeStruct((plan.rows, plan.cols), f32),
             jax.ShapeDtypeStruct((taps, width), f32),
-            jax.ShapeDtypeStruct((1, width), f32),
-            jax.ShapeDtypeStruct((1, width), f32),
+            jax.ShapeDtypeStruct((width,), f32),
+            jax.ShapeDtypeStruct((width,), f32),
         ),
         in_specs=[smem, vmem, vmem, vmem, vmem, anywhere, anywhere],
         out_specs=(anywhere, vmem, vmem, vmem, vmem),
@@ -441,8 +483,8 @@
         compiler_params=pltpu.CompilerParams(
             collective_id=0, has_side_effects=True, vmem_limit_bytes=60 * 1024 * 1024
         ),
-    )(lengths, pre_glu, kernel, bn_gain[None], bn_shift[None], w_out, cotangent)
-    return grad_pre, weight, kernel_grad, gain_grad[0], shift_grad[0]
+    )(lengths, pre_glu, kernel, bn_gain, bn_shift, w_out, cotangent)
+    return grad_pre, weight, kernel_grad, gain_grad, shift_grad
 
 
 def solution(mesh):

time: 92.7 us -> 77 us (0.83)
  Pallas kernels: 81.8 us -> 70.3 us
  other arithmetic: 2.62 us -> 0 us
  local copies, waits for them, and re-layouts: 6.63 us -> 5.24 us
    pallas_call x1, Pallas kernels: 81.8 us -> 70.3 us  [on_device(): pl.pallas_call(functools.partial(module_kernel, plan, sems), out_shape=(j...]
    pallas_call x2 -> x0, other arithmetic: 2.62 us -> none  [on_device(): pl.pallas_call(functools.partial(module_kernel, plan, sems), out_shape=(j...]
    broadcast_in_dim x2 -> x0, local copies, waits for them, and re-layouts: 2.59 us -> none  [the longest x1 1.3 us: on_device(): bn_gain[None]]
    unnamed x7 -> x13, local copies, waits for them, and re-layouts: 4.04 us -> 5.24 us
where the time goes in v2:
time: 77 us; the launch traced here: 76.9 us
  Pallas kernels  70.3 us (91%)
  local copies, waits for them, and re-layouts  5.24 us (7%)
  between operations  1.32 us (2%)
    pallas_call x1, Pallas kernels, on_device(): pl.pallas_call(functools.partial(module_kernel, plan, sems), out_shape=(j...  70.3 us
    unnamed x13, local copies, waits for them, and re-layouts  5.24 us

profile of v2, /device:TPU:0, one launch (start us, length us, event | category | flops | bytes accessed | tf_op | source)
XLA Modules:
  0.0 76.9 jit_solution(5415212026328334523)
XLA Ops:
  1.3 70.3 %shard_map.110 = (bf16[1,256,3072]{2,1,0:T(8,128)(2,1)}, f32[96,768]{1,0:T(8,128)}, f32[5,1536]{1,0:T(8,128)}, f32[1536]{0:T(1024)}, f32[1536]{0:T(1024)}) custom-call(s32[1]{0:T(128)S(6)} %copy.17.refs_0_, bf16[1,256,3072]{2,1,0:T(8,128)(2,1)} %refs_1_.1, f32[5,1536]{1,0:T(8,128)} %refs_2_.1, f32[1536]{0:T(1024)} %refs_3_.1, f32[1536]{0:T(1024)} %refs_4_.1, ...), custom_call_target="tpu_custom_call" | custom-call | tf_op jit(solution)/shard_map/pallas_call | solution.py:458
  71.6 0.0 copy-start
  71.6 0.0 copy-start.1
  71.6 0.0 copy-start.3
  71.6 0.0 copy-start.2
  71.6 2.7 %copy.18 = bf16[1,256,3072]{2,1,0:T(8,128)(2,1)} copy(bf16[1,256,3072]{2,1,0:T(8,128)(2,1)} %get-tuple-element.10) | data formatting | bytes 3145728
  74.3 0.0 copy-done
  74.3 0.7 copy.19
  75.0 0.0 copy-done.1
  75.0 0.6 copy.20
  75.7 0.0 copy-done.3
  75.7 0.6 copy.21
  76.3 0.0 copy-done.2
  76.3 0.6 copy.22
Async XLA Ops:
  71.6 2.7 %copy-start = (f32[96,768]{1,0:T(8,128)S(1)}, f32[96,768]{1,0:T(8,128)}, u32[]{:S(2)}) copy-start(f32[96,768]{1,0:T(8,128)} %get-tuple-element.11) | copy-start | bytes 884740
  71.6 3.4 %copy-start.1 = (f32[5,1536]{1,0:T(8,128)S(1)}, f32[5,1536]{1,0:T(8,128)}, u32[]{:S(2)}) copy-start(f32[5,1536]{1,0:T(8,128)} %get-tuple-element.12) | copy-start | bytes 92164
  71.6 4.1 %copy-start.3 = (f32[1536]{0:T(1024)S(1)}, f32[1536]{0:T(1024)}, u32[]{:S(2)}) copy-start(f32[1536]{0:T(1024)} %get-tuple-element.13) | copy-start | bytes 18436
  71.6 4.6 %copy-start.2 = (f32[1536]{0:T(1024)S(1)}, f32[1536]{0:T(1024)}, u32[]{:S(2)}) copy-start(f32[1536]{0:T(1024)} %get-tuple-element.14) | copy-start | bytes 18436
